TPU v7x, 32 devices: a whole 2x2x4 slice. The times are simulated.
32 devices in a mesh: ta: 4 (over x, core), ha: 4 (over z), wa: 2 (over y).
Axes of the slice: x: 2, y: 2, z: 4, core: 2. Of those that a mesh axis runs over, the one named last changes fastest.
Arguments:
- tokens: bfloat16 [1, 16, 32, 16, 1024], P(None, 'ta', 'ha', 'wa'), may hold values from -40 to 40
- norm_gain: float32 [4, 1024], replicated, may hold values from 0.25 to 1.75
- qkv_weight: bfloat16 [3, 1024, 3, 1024], P(None, None, None, 'ta'), may hold values from -0.1875 to 0.1875
- qk_gain: float32 [3, 2, 64], replicated, may hold values from 0.25 to 1.75
- out_weight: bfloat16 [3, 1024, 1024], P(None, 'ta'), may hold values from -0.1875 to 0.1875
- ffn_in: bfloat16 [1024, 2, 2048], P(None, None, 'ta'), may hold values from -0.1875 to 0.1875
- ffn_out: bfloat16 [2048, 1024], P('ta'), may hold values from -0.125 to 0.125
Outputs:
- layer_out: bfloat16 [1, 16, 32, 16, 1024], P(None, 'ta', 'ha', 'wa')
All inputs are finite; a program needn't handle non-finite values.
Results may differ from a plain program's by a relative error of at most 0.015.
Values may be sent and summed in bfloat16 or wider, within the bound.
A program may use at most 192 MiB of HBM per device.

v0:
```python
import functools

import jax
import jax.numpy as jnp
from jax import lax
from jax.experimental import pallas as pl
from jax.experimental.pallas import tpu as pltpu
from jax.sharding import PartitionSpec as P

HEAD_DIM = 64
EPS = 1e-06
MESH = pl.DeviceIdType.MESH
F32 = jnp.float32
BF16 = jnp.bfloat16


def dot(a, b):
    return jnp.dot(a, b, preferred_element_type=F32)


def dot_t(a, b):
    return lax.dot_general(a, b, (((1,), (1,)), ((), ())), preferred_element_type=F32)


def mask_of(cond_rows, cond_cols):
    return cond_rows == cond_cols


def attend(queries, key_rows, values, mask):
    width = queries.shape[-1]
    lane_head = lax.broadcasted_iota(jnp.int32, (1, width), 1) // HEAD_DIM
    total = None
    for head in range(width // HEAD_DIM):
        pick = (lane_head == head).astype(F32).astype(BF16)
        scores = dot_t(queries * pick, key_rows)
        weights = jnp.where(mask, jnp.exp(scores), 0.0)
        probs = weights * (1.0 / jnp.sum(weights, axis=-1, keepdims=True))
        part = dot(probs.astype(BF16), values * pick)
        total = part if total is None else total + part
    return total.astype(BF16)


class Plan:
    def __init__(self, n, n_ta, frames, rows):
        self.n = n
        self.m = min(n, frames)
        self.unit = rows // self.m
        self.u = n_ta * self.m // n


def kernel(cfg, tok, gain, qkg, wq_h, wo_h, wi_h, wf_h, out, *s):
    n_ta, frames, height, width, plans = cfg
    (stream, gath, wq, wo, wi, wf, pk, a0, a1, res0, res1, att, pk2, att2, pbuf, prec, comb, xrec,
     wsem, ag_s, ag_r, s10, r10, s20, r20, s11, r11, s21, r21, rs_s, rs_r) = s
    rows = tok.shape[0]
    per_frame = height * width
    aw = wo.shape[1]
    me = lax.axis_index("ta")
    core, chip = lax.rem(me, 2), lax.div(me, 2)

    def block_at(k):
        return lax.rem(chip + lax.div(k, 2), 2) * 2 + lax.rem(core + lax.rem(k, 2), 2)

    partner = block_at(1)
    remote = block_at(2)
    pair_last = block_at(3)

    copies = []
    for at in range(3):
        copies.append(pltpu.make_async_copy(wq_h.at[at], wq.at[at], wsem.at[at]))
        copies.append(pltpu.make_async_copy(wo_h.at[at], wo.at[at], wsem.at[3 + at]))
    copies.append(pltpu.make_async_copy(wi_h, wi, wsem.at[6]))
    copies.append(pltpu.make_async_copy(wf_h, wf, wsem.at[7]))
    for copy in copies:
        copy.start()

    barrier = pltpu.get_barrier_semaphore()
    greets = 0
    for other in (partner, remote):
        pl.semaphore_signal(barrier, inc=1, device_id={"ta": other}, device_id_type=MESH)
        greets += 1
    for axis, plan in plans:
        here = lax.axis_index(axis)
        for step in range(1, plan.n):
            other = lax.rem(here + step, plan.n)
            pl.semaphore_signal(barrier, inc=1, device_id={axis: other}, device_id_type=MESH)
            greets += 1

    def remote_copy(src, dst, send, recv, axis, other):
        return pltpu.make_async_remote_copy(
            src_ref=src, dst_ref=dst, send_sem=send, recv_sem=recv,
            device_id={axis: other}, device_id_type=MESH)

    def norm_own(p):
        x = stream[...]
        scale = lax.rsqrt(jnp.mean(x * x, axis=-1, keepdims=True) + EPS)
        gath[p, me] = (x * scale * gain[p:p + 1, :]).astype(BF16)

    def ag_copy(p, slot):
        block = me if slot < 2 else remote
        other = remote if slot == 1 else partner
        ref = gath.at[p, block]
        return remote_copy(ref, ref, ag_s.at[p, slot], ag_r.at[p, slot], "ta", other)

    def ag_start(p):
        ag_copy(p, 1).start()
        ag_copy(p, 0).start()

    def ag_wait(p, k):
        @pl.when(k == 1)
        def _():
            ag_copy(p, 0).wait_recv()

        @pl.when(k == 2)
        def _():
            ag_copy(p, 1).wait_recv()
            ag_copy(p, 2).start()

        @pl.when(k == 3)
        def _():
            ag_copy(p, 2).wait_recv()

    lane_a = lax.broadcasted_iota(jnp.int32, (aw, aw), 0) // HEAD_DIM
    lane_b = lax.broadcasted_iota(jnp.int32, (aw, aw), 1) // HEAD_DIM
    ones = (lane_a == lane_b).astype(F32).astype(BF16)

    def head_norm(x, row):
        square = x * x
        high = square.astype(BF16)
        low = (square - high.astype(F32)).astype(BF16)
        mean = (dot(high, ones) + dot(low, ones)) * (1.0 / HEAD_DIM)
        return x * lax.rsqrt(mean + EPS) * qkg[row:row + 1, :]

    def project(p, b):
        flat = dot(gath[p, b], wq[p])
        queries = (head_norm(flat[:, :aw], 2 * p) * (HEAD_DIM ** -0.5)).astype(BF16)
        key_rows = head_norm(flat[:, aw:2 * aw], 2 * p + 1).astype(BF16)
        return queries, key_rows, flat[:, 2 * aw:].astype(BF16)

    def rs_copy(p, slot):
        if slot == 0:
            return remote_copy(pbuf.at[p, 1], prec.at[p, 0], rs_s.at[p, 0], rs_r.at[p, 0], "ta", partner)
        if slot == 1:
            return remote_copy(pbuf.at[p, 3], prec.at[p, 1], rs_s.at[p, 1], rs_r.at[p, 1], "ta", partner)
        return remote_copy(comb.at[p], xrec.at[p], rs_s.at[p, 2], rs_r.at[p, 2], "ta", remote)

    def rs_put(p, k, part):
        pbuf[p, k] = part.astype(BF16)

        @pl.when(k == 1)
        def _():
            rs_copy(p, 0).start()

        @pl.when(k == 3)
        def _():
            rs_copy(p, 1).start()

    def rs_combine(p):
        rs_copy(p, 1).wait_recv()
        comb[p] = (pbuf[p, 2].astype(F32) + prec[p, 1].astype(F32)).astype(BF16)
        rs_copy(p, 2).start()

    def rs_total(p):
        rs_copy(p, 0).wait_recv()
        near = pbuf[p, 0].astype(F32) + prec[p, 0].astype(F32)
        rs_copy(p, 2).wait_recv()
        return stream[...] + (near + xrec[p].astype(F32))

    stream[...] = tok[...].astype(F32)
    norm_own(0)
    pl.semaphore_wait(barrier, greets)
    ag_start(0)

    sends = []
    for p in (0, 1):
        axis, plan = plans[p]
        n, m, unit, groups = plan.n, plan.m, plan.unit, plan.u
        here = lax.axis_index(axis)
        abuf, res = ((a0, res0), (a1, res1))[p]
        s1, r1, s2, r2 = ((s10, r10, s20, r20), (s11, r11, s21, r21))[p]
        if p:
            norm_own(p)
            ag_start(p)
        copies[2 * p].wait()

        def unit_copy(b, j, p=p, axis=axis, m=m, unit=unit, groups=groups, here=here, abuf=abuf, s1=s1, r1=r1):
            owner = j + m * lax.div(b, groups)
            u = lax.rem(b, groups)
            return owner, u, remote_copy(
                pk.at[p, b, pl.ds(j * unit, unit)], abuf.at[u, here], s1.at[b, j], r1.at[u, here], axis, owner)

        def first(k, _, p=p, m=m, unit=unit, here=here, abuf=abuf, unit_copy=unit_copy):
            b = block_at(k)
            ag_wait(p, k)
            queries, key_rows, values = project(p, b)
            pk[p, b, :, 0:aw] = queries
            pk[p, b, :, aw:2 * aw] = key_rows
            pk[p, b, :, 2 * aw:3 * aw] = values
            for j in range(m):
                owner, u, copy = unit_copy(b, j)

                @pl.when(owner != here)
                def _():
                    copy.start()

                @pl.when(owner == here)
                def _():
                    abuf[u, here] = pk[p, b, j * unit:(j + 1) * unit, :]
            return 0

        lax.fori_loop(0, n_ta, first, 0)

        size = n * unit
        if p == 0:
            line_of = lambda at: lax.div(lax.rem(at, unit), width)
        else:
            line_of = lambda at: lax.div(lax.rem(at, unit), per_frame) * width + lax.rem(at, width)
        mask = line_of(lax.broadcasted_iota(jnp.int32, (size, 1), 0)) == line_of(
            lax.broadcasted_iota(jnp.int32, (1, size), 1))

        def back_copy(u, other, p=p, axis=axis, m=m, unit=unit, groups=groups, here=here, res=res, s2=s2, r2=r2):
            j = lax.rem(here, m)
            b = u + groups * lax.div(here, m)
            return remote_copy(
                res.at[u, other], att.at[p, b, pl.ds(pl.multiple_of(j * unit, unit), unit)],
                s2.at[u, other], r2.at[b, j], axis, other)

        def second(k, _, p=p, axis=axis, n=n, m=m, unit=unit, groups=groups, here=here, abuf=abuf, res=res,
                   r1=r1, s1=s1, mask=mask, size=size, back_copy=back_copy):
            u = lax.rem(block_at(k), groups)
            for step in range(1, n):
                source = lax.rem(here + step, n)
                remote_copy(abuf.at[u, source], abuf.at[u, source], s1.at[0, 0], r1.at[u, source],
                            axis, source).wait_recv()
            done = attend(
                abuf[u, :, :, 0:aw].reshape(size, aw),
                abuf[u, :, :, aw:2 * aw].reshape(size, aw),
                abuf[u, :, :, 2 * aw:3 * aw].reshape(size, aw),
                mask,
            )
            res[u] = done.reshape(n, unit, aw)
            for step in range(1, n):
                back_copy(u, lax.rem(here + step, n)).start()
            j = lax.rem(here, m)
            b = u + groups * lax.div(here, m)
            att[p, b, pl.ds(pl.multiple_of(j * unit, unit), unit)] = res[u, here]
            return 0

        lax.fori_loop(0, groups, second, 0)
        copies[2 * p + 1].wait()

        def third(i, _, p=p, axis=axis, m=m, unit=unit, groups=groups, here=here, s2=s2, r2=r2):
            k = n_ta - 1 - i
            b = block_at(k)
            for j in range(m):
                owner = j + m * lax.div(b, groups)

                @pl.when(owner != here)
                def _():
                    ref = att.at[p, b, pl.ds(j * unit, unit)]
                    remote_copy(ref, ref, s2.at[0, 0], r2.at[b, j], axis, owner).wait_recv()
            rs_put(p, k, dot(att[p, b], wo[p]))

            @pl.when(k == 2)
            def _():
                rs_combine(p)
            return 0

        lax.fori_loop(0, n_ta, third, 0)
        stream[...] = rs_total(p)

        def drain(unit_copy=unit_copy, back_copy=back_copy, n=n, m=m, groups=groups, here=here):
            for b in range(n_ta):
                for j in range(m):
                    owner, _, copy = unit_copy(b, j)

                    @pl.when(owner != here)
                    def _():
                        copy.wait_send()
            for u in range(groups):
                for step in range(1, n):
                    back_copy(u, lax.rem(here + step, n)).wait_send()

        sends.append(drain)

    p = 2
    norm_own(p)
    ag_start(p)
    copies[2 * p].wait()

    def time_first(k, _):
        b = block_at(k)
        ag_wait(p, k)
        queries, key_rows, values = project(p, b)
        at = pl.ds(b * frames, frames)
        pk2[at, :, 0:aw] = queries.reshape(frames, per_frame, aw)
        pk2[at, :, aw:2 * aw] = key_rows.reshape(frames, per_frame, aw)
        pk2[at, :, 2 * aw:3 * aw] = values.reshape(frames, per_frame, aw)
        return 0

    lax.fori_loop(0, n_ta, time_first, 0)
    every = n_ta * frames
    some = 16
    size = every * some
    i_at = lax.broadcasted_iota(jnp.int32, (size, 1), 0)
    j_at = lax.broadcasted_iota(jnp.int32, (1, size), 1)
    causal = (lax.rem(i_at, some) == lax.rem(j_at, some)) & (lax.div(i_at, some) >= lax.div(j_at, some))

    def time_second(g, _):
        at = pl.ds(pl.multiple_of(g * some, some), some)
        done = attend(
            pk2[:, at, 0:aw].reshape(size, aw),
            pk2[:, at, aw:2 * aw].reshape(size, aw),
            pk2[:, at, 2 * aw:3 * aw].reshape(size, aw),
            causal,
        )
        att2[:, at, :] = done.reshape(every, some, aw)
        return 0

    lax.fori_loop(0, per_frame // some, time_second, 0)
    copies[2 * p + 1].wait()

    def time_third(i, _):
        k = n_ta - 1 - i
        b = block_at(k)
        rs_put(p, k, dot(att2[pl.ds(b * frames, frames)].reshape(rows, aw), wo[p]))

        @pl.when(k == 2)
        def _():
            rs_combine(p)
        return 0

    lax.fori_loop(0, n_ta, time_third, 0)
    stream[...] = rs_total(p)

    norm_own(3)
    ag_start(3)
    copies[6].wait()
    copies[7].wait()
    half = wf.shape[0]

    def mlp(k, _):
        b = block_at(k)
        ag_wait(3, k)
        both = dot(gath[3, b], wi[...])
        gate, up = both[:, :half], both[:, half:]
        hidden = (gate / (1.0 + jnp.exp(-gate)) * up).astype(BF16)
        rs_put(3, k, dot(hidden, wf[...]))
        return 0

    lax.fori_loop(0, n_ta, mlp, 0)
    rs_combine(3)
    out[...] = rs_total(3).astype(BF16)

    for drain in sends:
        drain()
    for p in range(4):
        for slot in range(3):
            ag_copy(p, slot).wait_send()
            rs_copy(p, slot).wait_send()


def local(sizes, tokens, norm_gain, qkv_weight, qk_gain, out_weight, ffn_in, ffn_out):
    n_ta, n_ha, n_wa = sizes
    extent = tokens.shape
    clips, frames, height, width, model = extent
    rows = clips * frames * height * width
    aw = qkv_weight.shape[-1]
    half = ffn_in.shape[-1]
    plans = (("wa", Plan(n_wa, n_ta, frames, rows)), ("ha", Plan(n_ha, n_ta, frames, rows)))
    cfg = (n_ta, frames, height, width, plans)
    heads = aw // HEAD_DIM
    gains = jnp.tile(qk_gain.reshape(-1, HEAD_DIM), (1, heads))
    dma = pltpu.SemaphoreType.DMA
    vm = pltpu.VMEM
    scratch = [
        vm((rows, model), F32),
        vm((4, n_ta, rows, model), BF16),
        vm((3, model, 3 * aw), BF16),
        vm((3, aw, model), BF16),
        vm((model, 2 * half), BF16),
        vm((half, model), BF16),
        vm((2, n_ta, rows, 3 * aw), BF16),
    ]
    for width_of in (3 * aw, aw):
        for _, plan in plans:
            scratch.append(vm((plan.u, plan.n, plan.unit, width_of), BF16))
    scratch += [
        vm((2, n_ta, rows, aw), BF16),
        vm((n_ta * frames, height * width, 3 * aw), BF16),
        vm((n_ta * frames, height * width, aw), BF16),
        vm((4, n_ta, rows, model), BF16),
        vm((4, 2, rows, model), BF16),
        vm((4, rows, model), BF16),
        vm((4, rows, model), BF16),
        dma((8,)),
        dma((4, 3)),
        dma((4, 3)),
    ]
    for _, plan in plans:
        scratch += [
            dma((n_ta, plan.m)),
            dma((plan.u, plan.n)),
            dma((plan.u, plan.n)),
            dma((n_ta, plan.m)),
        ]
    scratch += [dma((4, 3)), dma((4, 3))]
    vmem = pl.BlockSpec(memory_space=pltpu.VMEM)
    anyw = pl.BlockSpec(memory_space=pl.ANY)
    result = pl.pallas_call(
        functools.partial(kernel, cfg),
        out_shape=jax.ShapeDtypeStruct((rows, model), BF16),
        in_specs=[vmem, vmem, vmem, anyw, anyw, anyw, anyw],
        out_specs=vmem,
        scratch_shapes=scratch,
        compiler_params=pltpu.CompilerParams(
            collective_id=0, has_side_effects=True, vmem_limit_bytes=67043328),
        name="axial_layer",
    )(
        tokens.reshape(rows, model),
        norm_gain,
        gains,
        qkv_weight.reshape(3, model, 3 * aw),
        out_weight,
        ffn_in.reshape(model, 2 * half),
        ffn_out,
    )
    return result.reshape(extent)


def solution(mesh):
    sizes = tuple(mesh.shape[name] for name in ("ta", "ha", "wa"))
    return jax.shard_map(
        functools.partial(local, sizes),
        mesh=mesh,
        in_specs=(
            P(None, "ta", "ha", "wa", None),
            P(),
            P(None, None, None, "ta"),
            P(),
            P(None, "ta", None),
            P(None, None, "ta"),
            P("ta", None),
        ),
        out_specs=P(None, "ta", "ha", "wa", None),
        check_vma=False,
    )
```

profile of v0, /device:TPU:0, one launch (start us, length us, event | category | flops | bytes accessed | tf_op | source)
XLA Modules:
  0.0 195.1 jit_solution(15334169081234547968)
XLA Ops:
  0.0 6.7 %copy.9 = bf16[3,1024,3,256]{1,3,2,0:T(8,128)(2,1)} copy(bf16[3,1024,3,256]{3,1,2,0:T(8,128)(2,1)} %param.9) | data formatting | bytes 9437184 | tf_op args[2]
  6.7 0.0 copy-start
  6.7 0.0 copy-start.1
  6.7 6.8 %copy.10.wq_h = bf16[3,1024,768]{2,1,0:T(8,128)(2,1)} copy(bf16[3,1024,768]{1,2,0:T(8,128)(2,1)} %bitcast.5) | data formatting | bytes 9437184 | tf_op jit(solution)/shard_map/reshape | solution.py:423
  13.5 0.0 copy-done
  13.5 2.0 %copy.11 = bf16[128,8,2,512]{3,1,2,0:T(8,128)(2,1)} copy(bf16[128,8,2,512]{3,2,1,0:T(2,128)(2,1)S(1)} %bitcast.8) | data formatting | bytes 4194304
  15.4 0.0 copy-done.1
  15.4 0.7 tile.12.qkg
  16.1 177.1 %axial_layer.1 = bf16[256,1024]{1,0:T(8,128)(2,1)} custom-call(bf16[256,1024]{1,0:T(8,128)(2,1)} %bitcast.9, f32[4,1024]{1,0:T(4,128)} %gain.1, f32[6,256]{1,0:T(8,128)} %tile.12.qkg, bf16[3,1024,768]{2,1,0:T(8,128)(2,1)} %copy.10.wq_h, bf16[3,256,1024]{2,1,0:T(8,128)(2,1)} %wo_h.1, bf16[1024,1024]{1,0:T(8,128)(2,1)} %bitcast.6, bf16[512,1024]{1,0:T(8,128)(2,1)} %wf_h.1), custom_call_target="tpu_custom_call" | custom-call | tf_op jit(solution)/shard_map/axial_layer/pallas_call | solution.py:410
  193.2 1.9 copy.13
  (2 shorter events, 0.0 us)
Async XLA Ops:
  6.7 6.8 %copy-start = (bf16[1024,2,512]{2,1,0:T(2,128)(2,1)S(1)}, bf16[1024,2,512]{2,1,0:T(2,128)(2,1)}, u32[]{:S(2)}) copy-start(bf16[1024,2,512]{2,1,0:T(2,128)(2,1)} %param.12) | copy-start | bytes 6291460
  6.7 8.7 %copy-start.1 = (f32[3,2,64]{2,1,0:T(2,128)S(1)}, f32[3,2,64]{2,1,0:T(2,128)}, u32[]{:S(2)}) copy-start(f32[3,2,64]{2,1,0:T(2,128)} %param.10) | copy-start | bytes 4612
where the time goes:
time: 195 us
  Pallas kernels  177 us (91%)
  local copies, waits for them, and re-layouts  18 us (9%)
    pallas_call x1, Pallas kernels, local(): pl.pallas_call(functools.partial(kernel, cfg), out_shape=jax.ShapeDtypeSt...  177 us
    unnamed x7, local copies, waits for them, and re-layouts  10.5 us
    reshape x1, local copies, waits for them, and re-layouts, local(): qkv_weight.reshape(3, model, 3 * aw)  6.78 us

commit v1 on v0

v1 whole, which is shorter than its diff:
```python
import functools

import jax
import jax.numpy as jnp
from jax import lax
from jax.experimental import pallas as pl
from jax.experimental.pallas import tpu as pltpu
from jax.sharding import PartitionSpec as P

HEAD_DIM = 64
CHUNKS = 2
EPS = 1e-06
MESH = pl.DeviceIdType.MESH
F32 = jnp.float32
BF16 = jnp.bfloat16


def dot(a, b):
    return jnp.dot(a, b, preferred_element_type=F32)


def dot_t(a, b):
    return lax.dot_general(a, b, (((1,), (1,)), ((), ())), preferred_element_type=F32)


def attend(queries, key_rows, values, mask):
    width = queries.shape[-1]
    lane_head = lax.broadcasted_iota(jnp.int32, (1, width), 1) // HEAD_DIM
    total = None
    for head in range(width // HEAD_DIM):
        pick = (lane_head == head).astype(F32).astype(BF16)
        scores = dot_t(queries * pick, key_rows)
        weights = jnp.where(mask, jnp.exp(scores), 0.0)
        probs = weights * (1.0 / jnp.sum(weights, axis=-1, keepdims=True))
        part = dot(probs.astype(BF16), values * pick)
        total = part if total is None else total + part
    return total.astype(BF16)


class Plan:
    def __init__(self, n, n_ta, frames, rows):
        self.n = n
        self.m = frames
        self.unit = rows // frames
        self.low = min(n, frames)
        self.q = frames // self.low
        self.blocks = n_ta * frames // max(n, frames)
        self.u = self.blocks * self.q


def kernel(cfg, tok, gain, qkg, wq_h, wo_h, wi_h, wf_h, out, *s):
    n_ta, frames, height, width, plans = cfg
    (stream, gath, wq, wo, wi, wf, pk, a0, a1, res0, res1, att, pk2, att2, pbuf, prec, comb, xrec,
     wsem, ag_s, ag_r, s10, r10, s20, r20, s11, r11, s21, r21, rs_s, rs_r) = s
    rows = tok.shape[0]
    per_frame = height * width
    aw = wo.shape[1]
    me = lax.axis_index("ta")
    core, chip = lax.rem(me, 2), lax.div(me, 2)

    def block_at(k):
        return lax.rem(chip + lax.div(k, 2), 2) * 2 + lax.rem(core + lax.rem(k, 2), 2)

    piece = rows // CHUNKS
    wide = lambda c: pl.ds(pl.multiple_of(c * piece, piece), piece)
    steps = n_ta * CHUNKS
    early = 2 * CHUNKS

    def arrival(i):
        late = i - early
        k = jnp.where(i < early, lax.div(i, CHUNKS), 2 + lax.rem(late, 2))
        c = jnp.where(i < early, lax.rem(i, CHUNKS), lax.div(late, 2))
        return k, c

    def departure(i):
        rest = i - early
        k = jnp.where(i < early, 3 - lax.rem(i, 2), 1 - lax.div(rest, CHUNKS))
        c = jnp.where(i < early, lax.div(i, 2), lax.rem(rest, CHUNKS))
        return k, c

    partner = block_at(1)
    remote = block_at(2)
    pair_last = block_at(3)

    copies = []
    for at in range(3):
        copies.append([
            pltpu.make_async_copy(wq_h.at[at, j], wq.at[at, :, j * aw:(j + 1) * aw], wsem.at[at, j])
            for j in range(3)])
        copies.append([pltpu.make_async_copy(wo_h.at[at], wo.at[at], wsem.at[at, 3])])
    copies.append([pltpu.make_async_copy(wi_h, wi, wsem.at[3, 0])])
    copies.append([pltpu.make_async_copy(wf_h, wf, wsem.at[3, 1])])
    for group in copies:
        for copy in group:
            copy.start()

    def ready(at):
        for copy in copies[at]:
            copy.wait()

    barrier = pltpu.get_barrier_semaphore()
    greets = 0
    for other in (partner, remote):
        pl.semaphore_signal(barrier, inc=1, device_id={"ta": other}, device_id_type=MESH)
        greets += 1
    for axis, plan in plans:
        here = lax.axis_index(axis)
        for step in range(1, plan.n):
            other = lax.rem(here + step, plan.n)
            pl.semaphore_signal(barrier, inc=1, device_id={axis: other}, device_id_type=MESH)
            greets += 1

    def remote_copy(src, dst, send, recv, axis, other):
        return pltpu.make_async_remote_copy(
            src_ref=src, dst_ref=dst, send_sem=send, recv_sem=recv,
            device_id={axis: other}, device_id_type=MESH)

    def norm_own(p, c):
        x = stream[wide(c), :]
        scale = lax.rsqrt(jnp.mean(x * x, axis=-1, keepdims=True) + EPS)
        gath[p, me, wide(c)] = (x * scale * gain[p:p + 1, :]).astype(BF16)

    def ag_copy(p, slot, c):
        block = me if slot < 2 else remote
        other = remote if slot == 1 else partner
        ref = gath.at[p, block, wide(c)]
        return remote_copy(ref, ref, ag_s.at[p, slot, c], ag_r.at[p, slot, c], "ta", other)

    def ag_start(p, c):
        ag_copy(p, 1, c).start()
        ag_copy(p, 0, c).start()

    def ag_wait(p, k, c):
        @pl.when(k == 1)
        def _():
            ag_copy(p, 0, c).wait_recv()

        @pl.when(k == 2)
        def _():
            ag_copy(p, 1, c).wait_recv()
            ag_copy(p, 2, c).start()

        @pl.when(k == 3)
        def _():
            ag_copy(p, 2, c).wait_recv()

    lane_a = lax.broadcasted_iota(jnp.int32, (aw, aw), 0) // HEAD_DIM
    lane_b = lax.broadcasted_iota(jnp.int32, (aw, aw), 1) // HEAD_DIM
    ones = (lane_a == lane_b).astype(F32).astype(BF16)

    def head_norm(x, row):
        square = x * x
        high = square.astype(BF16)
        low = (square - high.astype(F32)).astype(BF16)
        mean = (dot(high, ones) + dot(low, ones)) * (1.0 / HEAD_DIM)
        return x * lax.rsqrt(mean + EPS) * qkg[row:row + 1, :]

    def project(p, b, c):
        flat = dot(gath[p, b, wide(c)], wq[p])
        queries = (head_norm(flat[:, :aw], 2 * p) * (HEAD_DIM ** -0.5)).astype(BF16)
        key_rows = head_norm(flat[:, aw:2 * aw], 2 * p + 1).astype(BF16)
        return queries, key_rows, flat[:, 2 * aw:].astype(BF16)

    def rs_copy(p, slot, c):
        send, recv = rs_s.at[p, slot, c], rs_r.at[p, slot, c]
        if slot == 2:
            return remote_copy(comb.at[p, wide(c)], xrec.at[p, wide(c)], send, recv, "ta", remote)
        return remote_copy(pbuf.at[p, 2 * slot + 1, wide(c)], prec.at[p, slot, wide(c)], send, recv, "ta", partner)

    def rs_put(p, k, c, part):
        pbuf[p, k, wide(c)] = part.astype(BF16)

        @pl.when(k == 1)
        def _():
            rs_copy(p, 0, c).start()

        @pl.when(k == 3)
        def _():
            rs_copy(p, 1, c).start()

    def rs_combine(p, c):
        rs_copy(p, 1, c).wait_recv()
        comb[p, wide(c)] = (pbuf[p, 2, wide(c)].astype(F32) + prec[p, 1, wide(c)].astype(F32)).astype(BF16)
        rs_copy(p, 2, c).start()

    def rs_total(p, c):
        rs_copy(p, 0, c).wait_recv()
        near = pbuf[p, 0, wide(c)].astype(F32) + prec[p, 0, wide(c)].astype(F32)
        rs_copy(p, 2, c).wait_recv()
        return stream[wide(c), :] + (near + xrec[p, wide(c)].astype(F32))

    def turn(p):
        for c in range(CHUNKS):
            stream[wide(c), :] = rs_total(p, c)
            norm_own(p + 1, c)
            ag_start(p + 1, c)

    stream[...] = tok[...].astype(F32)
    norm_own(0, 0)
    pl.semaphore_wait(barrier, greets)
    ag_start(0, 0)
    for c in range(1, CHUNKS):
        norm_own(0, c)
        ag_start(0, c)

    sends = []
    for p in (0, 1):
        axis, plan = plans[p]
        n, m, unit, groups, low, fold, span = plan.n, plan.m, plan.unit, plan.u, plan.low, plan.q, plan.blocks
        here = lax.axis_index(axis)
        abuf, res = ((a0, res0), (a1, res1))[p]
        s1, r1, s2, r2 = ((s10, r10, s20, r20), (s11, r11, s21, r21))[p]
        ready(2 * p)

        def owner_of(b, j, m=m, low=low, span=span):
            return lax.rem(j, low) + m * lax.div(b, span)

        def place(j, unit=unit):
            return pl.ds(pl.multiple_of(j * unit, unit), unit)

        def unit_copy(b, j, p=p, axis=axis, low=low, fold=fold, span=span, here=here, abuf=abuf, s1=s1, r1=r1,
                      owner_of=owner_of, place=place):
            owner = owner_of(b, j)
            u = lax.rem(b, span) * fold + lax.div(j, low)
            return owner, u, remote_copy(
                pk.at[p, b, place(j)], abuf.at[u, here], s1.at[b, j], r1.at[u, here], axis, owner)

        def first(i, _, p=p, m=m, here=here, abuf=abuf, unit_copy=unit_copy, place=place):
            k, c = arrival(i)
            b = block_at(k)
            ag_wait(p, k, c)
            queries, key_rows, values = project(p, b, c)
            pk[p, b, wide(c), 0:aw] = queries
            pk[p, b, wide(c), aw:2 * aw] = key_rows
            pk[p, b, wide(c), 2 * aw:3 * aw] = values
            for at in range(m // CHUNKS):
                j = c * (m // CHUNKS) + at
                owner, u, copy = unit_copy(b, j)

                @pl.when(owner != here)
                def _():
                    copy.start()

                @pl.when(owner == here)
                def _():
                    abuf[u, here] = pk[p, b, place(j), :]
            return 0

        lax.fori_loop(0, steps, first, 0)

        size = n * unit
        if p == 0:
            line_of = lambda at: lax.div(lax.rem(at, unit), width)
        else:
            line_of = lambda at: lax.div(lax.rem(at, unit), per_frame) * width + lax.rem(at, width)
        mask = line_of(lax.broadcasted_iota(jnp.int32, (size, 1), 0)) == line_of(
            lax.broadcasted_iota(jnp.int32, (1, size), 1))

        def home(u, m=m, low=low, fold=fold, span=span, here=here):
            return lax.div(u, fold) + span * lax.div(here, m), lax.rem(here, low) + low * lax.rem(u, fold)

        def back_copy(u, other, p=p, axis=axis, res=res, s2=s2, r2=r2, home=home, place=place):
            b, j = home(u)
            return remote_copy(
                res.at[u, other], att.at[p, b, place(j)], s2.at[u, other], r2.at[b, j], axis, other)

        def second(i, _, p=p, axis=axis, n=n, unit=unit, fold=fold, span=span, here=here, abuf=abuf, res=res,
                   r1=r1, s1=s1, mask=mask, size=size, back_copy=back_copy, home=home, place=place):
            k, sub = arrival(i) if fold == CHUNKS else (lax.div(i, fold), lax.rem(i, fold))
            u = lax.rem(block_at(k), span) * fold + sub
            for step in range(1, n):
                source = lax.rem(here + step, n)
                remote_copy(abuf.at[u, source], abuf.at[u, source], s1.at[0, 0], r1.at[u, source],
                            axis, source).wait_recv()
            done = attend(
                abuf[u, :, :, 0:aw].reshape(size, aw),
                abuf[u, :, :, aw:2 * aw].reshape(size, aw),
                abuf[u, :, :, 2 * aw:3 * aw].reshape(size, aw),
                mask,
            )
            res[u] = done.reshape(n, unit, aw)
            for step in range(1, n):
                back_copy(u, lax.rem(here + step, n)).start()
            b, j = home(u)
            att[p, b, place(j)] = res[u, here]
            return 0

        lax.fori_loop(0, groups, second, 0)
        ready(2 * p + 1)

        def third(i, _, p=p, axis=axis, m=m, here=here, s2=s2, r2=r2, owner_of=owner_of, place=place):
            k, c = departure(i)
            b = block_at(k)
            for at in range(m // CHUNKS):
                j = c * (m // CHUNKS) + at
                owner = owner_of(b, j)

                @pl.when(owner != here)
                def _():
                    ref = att.at[p, b, place(j)]
                    remote_copy(ref, ref, s2.at[0, 0], r2.at[b, j], axis, owner).wait_recv()
            rs_put(p, k, c, dot(att[p, b, wide(c)], wo[p]))

            @pl.when(k == 2)
            def _():
                rs_combine(p, c)
            return 0

        lax.fori_loop(0, steps, third, 0)
        turn(p)

        def drain(unit_copy=unit_copy, back_copy=back_copy, n=n, m=m, groups=groups, here=here):
            for b in range(n_ta):
                for j in range(m):
                    owner, _, copy = unit_copy(b, j)

                    @pl.when(owner != here)
                    def _():
                        copy.wait_send()
            for u in range(groups):
                for step in range(1, n):
                    back_copy(u, lax.rem(here + step, n)).wait_send()

        sends.append(drain)

    p = 2
    some_frames = frames // CHUNKS
    ready(2 * p)

    def time_first(i, _):
        k, c = arrival(i)
        b = block_at(k)
        ag_wait(p, k, c)
        queries, key_rows, values = project(p, b, c)
        at = pl.ds(b * frames + c * some_frames, some_frames)
        pk2[at, :, 0:aw] = queries.reshape(some_frames, per_frame, aw)
        pk2[at, :, aw:2 * aw] = key_rows.reshape(some_frames, per_frame, aw)
        pk2[at, :, 2 * aw:3 * aw] = values.reshape(some_frames, per_frame, aw)
        return 0

    lax.fori_loop(0, steps, time_first, 0)
    every = n_ta * frames
    some = 16
    size = every * some
    i_at = lax.broadcasted_iota(jnp.int32, (size, 1), 0)
    j_at = lax.broadcasted_iota(jnp.int32, (1, size), 1)
    causal = (lax.rem(i_at, some) == lax.rem(j_at, some)) & (lax.div(i_at, some) >= lax.div(j_at, some))

    def time_second(g, _):
        at = pl.ds(pl.multiple_of(g * some, some), some)
        done = attend(
            pk2[:, at, 0:aw].reshape(size, aw),
            pk2[:, at, aw:2 * aw].reshape(size, aw),
            pk2[:, at, 2 * aw:3 * aw].reshape(size, aw),
            causal,
        )
        att2[:, at, :] = done.reshape(every, some, aw)
        return 0

    lax.fori_loop(0, per_frame // some, time_second, 0)
    ready(2 * p + 1)

    def time_third(i, _):
        k, c = departure(i)
        b = block_at(k)
        at = pl.ds(b * frames + c * some_frames, some_frames)
        rs_put(p, k, c, dot(att2[at].reshape(piece, aw), wo[p]))

        @pl.when(k == 2)
        def _():
            rs_combine(p, c)
        return 0

    lax.fori_loop(0, steps, time_third, 0)
    turn(p)

    ready(6)
    ready(7)
    half = wf.shape[0]

    def mlp(i, _):
        k, c = arrival(i)
        b = block_at(k)
        ag_wait(3, k, c)
        both = dot(gath[3, b, wide(c)], wi[...])
        gate, up = both[:, :half], both[:, half:]
        hidden = (gate / (1.0 + jnp.exp(-gate)) * up).astype(BF16)
        rs_put(3, k, c, dot(hidden, wf[...]))

        @pl.when((k == 2) & (c > 0))
        def _():
            rs_combine(3, c - 1)
        return 0

    lax.fori_loop(0, steps, mlp, 0)
    rs_combine(3, CHUNKS - 1)
    for c in range(CHUNKS):
        out[wide(c), :] = rs_total(3, c).astype(BF16)

    for drain in sends:
        drain()
    for p in range(4):
        for slot in range(3):
            for c in range(CHUNKS):
                ag_copy(p, slot, c).wait_send()
                rs_copy(p, slot, c).wait_send()


def local(sizes, tokens, norm_gain, qkv_weight, qk_gain, out_weight, ffn_in, ffn_out):
    n_ta, n_ha, n_wa = sizes
    extent = tokens.shape
    clips, frames, height, width, model = extent
    rows = clips * frames * height * width
    aw = qkv_weight.shape[-1]
    half = ffn_in.shape[-1]
    plans = (("wa", Plan(n_wa, n_ta, frames, rows)), ("ha", Plan(n_ha, n_ta, frames, rows)))
    cfg = (n_ta, frames, height, width, plans)
    heads = aw // HEAD_DIM
    gains = jnp.tile(qk_gain.reshape(-1, HEAD_DIM), (1, heads))
    dma = pltpu.SemaphoreType.DMA
    vm = pltpu.VMEM
    scratch = [
        vm((rows, model), F32),
        vm((4, n_ta, rows, model), BF16),
        vm((3, model, 3 * aw), BF16),
        vm((3, aw, model), BF16),
        vm((model, 2 * half), BF16),
        vm((half, model), BF16),
        vm((2, n_ta, rows, 3 * aw), BF16),
    ]
    for width_of in (3 * aw, aw):
        for _, plan in plans:
            scratch.append(vm((plan.u, plan.n, plan.unit, width_of), BF16))
    scratch += [
        vm((2, n_ta, rows, aw), BF16),
        vm((n_ta * frames, height * width, 3 * aw), BF16),
        vm((n_ta * frames, height * width, aw), BF16),
        vm((4, n_ta, rows, model), BF16),
        vm((4, 2, rows, model), BF16),
        vm((4, rows, model), BF16),
        vm((4, rows, model), BF16),
        dma((4, 4)),
        dma((4, 3, CHUNKS)),
        dma((4, 3, CHUNKS)),
    ]
    for _, plan in plans:
        scratch += [
            dma((n_ta, plan.m)),
            dma((plan.u, plan.n)),
            dma((plan.u, plan.n)),
            dma((n_ta, plan.m)),
        ]
    scratch += [dma((4, 3, CHUNKS)), dma((4, 3, CHUNKS))]
    vmem = pl.BlockSpec(memory_space=pltpu.VMEM)
    anyw = pl.BlockSpec(memory_space=pl.ANY)
    result = pl.pallas_call(
        functools.partial(kernel, cfg),
        out_shape=jax.ShapeDtypeStruct((rows, model), BF16),
        in_specs=[vmem, vmem, vmem, anyw, anyw, anyw, anyw],
        out_specs=vmem,
        scratch_shapes=scratch,
        compiler_params=pltpu.CompilerParams(
            collective_id=0, has_side_effects=True, vmem_limit_bytes=67043328),
        name="axial_layer",
    )(
        tokens.reshape(rows, model),
        norm_gain,
        gains,
        jnp.transpose(qkv_weight, (0, 2, 1, 3)),
        out_weight,
        ffn_in.reshape(model, 2 * half),
        ffn_out,
    )
    return result.reshape(extent)


def solution(mesh):
    sizes = tuple(mesh.shape[name] for name in ("ta", "ha", "wa"))
    return jax.shard_map(
        functools.partial(local, sizes),
        mesh=mesh,
        in_specs=(
            P(None, "ta", "ha", "wa", None),
            P(),
            P(None, None, None, "ta"),
            P(),
            P(None, "ta", None),
            P(None, None, "ta"),
            P("ta", None),
        ),
        out_specs=P(None, "ta", "ha", "wa", None),
        check_vma=False,
    )
```

time: 195 us -> 171 us (0.88); the launches traced: 195 us -> 169 us
  Pallas kernels: 177 us -> 162 us
  local copies, waits for them, and re-layouts: 18 us -> 6.76 us
    pallas_call x1, Pallas kernels: 177 us -> 162 us  [local(): pl.pallas_call(functools.partial(kernel, cfg), out_shape=jax.ShapeDtypeSt...]
    reshape x1 -> x0, local copies, waits for them, and re-layouts: 6.78 us -> none  [local(): qkv_weight.reshape(3, model, 3 * aw)]
    unnamed x7 -> x2, local copies, waits for them, and re-layouts: 10.5 us -> 5.38 us
where the time goes in v1:
time: 171 us; the launch traced here: 169 us
  Pallas kernels  162 us (95%)
  local copies, waits for them, and re-layouts  6.76 us (4%)
    pallas_call x1, Pallas kernels, local(): pl.pallas_call(functools.partial(kernel, cfg), out_shape=jax.ShapeDtypeSt...  162 us
    unnamed x2, local copies, waits for them, and re-layouts  5.38 us

profile of v1, /device:TPU:0, one launch (start us, length us, event | category | flops | bytes accessed | tf_op | source)
XLA Modules:
  0.0 168.6 jit_solution(9361787357970013044)
XLA Ops:
  0.0 0.7 tile.10
  0.7 0.7 tile.12.qkg
  1.4 3.5 %copy.8 = bf16[128,8,2,512]{3,1,2,0:T(8,128)(2,1)} copy(bf16[128,8,2,512]{3,2,1,0:T(2,128)(2,1)} %bitcast.8) | data formatting | bytes 4194304
  4.9 161.9 %axial_layer.1 = bf16[256,1024]{1,0:T(8,128)(2,1)} custom-call(bf16[256,1024]{1,0:T(8,128)(2,1)} %bitcast.9, f32[4,1024]{1,0:T(4,128)} %gain.1, f32[6,256]{1,0:T(8,128)} %tile.12.qkg, bf16[3,3,1024,256]{3,2,1,0:T(8,128)(2,1)} %bitcast.6, bf16[3,256,1024]{2,1,0:T(8,128)(2,1)} %wo_h.1, bf16[1024,1024]{1,0:T(8,128)(2,1)} %bitcast.5, bf16[512,1024]{1,0:T(8,128)(2,1)} %wf_h.1), custom_call_target="tpu_custom_call" | custom-call | tf_op jit(solution)/shard_map/axial_layer/pallas_call | solution.py:456
  166.8 1.9 %copy.10 = bf16[1,4,8,8,1024]{4,3,2,1,0:T(8,128)(2,1)} copy(bf16[1,4,8,8,1024]{4,3,2,1,0:T(8,128)(2,1)} %bitcast.7) | data formatting | bytes 1048576
  (1 shorter events, 0.0 us)
